TPU v7x, 32 devices: a whole 2x2x4 slice. The times are simulated.
32 devices in a mesh: blk: 8 (over y, x, core), uly: 1, dp: 4 (over z).
Axes of the slice: x: 2, y: 2, z: 4, core: 2. Of those that a mesh axis runs over, the one named last changes fastest.
Arguments:
- short_tokens: bfloat16 [32, 1024, 4096], P(('blk', 'dp'), 'uly'), may hold values from -150 to 150, as said below
- short_segments: int32 [32, 1024], P(('blk', 'dp')), may hold values from 0 to 3, never falling along the last dimension, each value on 1 to 512 neighbouring positions
- long_tokens: bfloat16 [4, 3072, 4096], P('dp', 'blk'), may hold values from -150 to 150, as said below
- long_lengths: int32 [4], P('dp'), may hold values from 768 to 3072
- w_query: bfloat16 [4096, 2048], P(('blk', 'dp'), 'uly'), may hold values from -0.09375 to 0.09375
- w_key: bfloat16 [4096, 512], P(('blk', 'dp'), 'uly'), may hold values from -0.09375 to 0.09375
- w_value: bfloat16 [4096, 512], P(('blk', 'dp'), 'uly'), may hold values from -0.09375 to 0.09375
Outputs:
- short_out: bfloat16 [32, 1024, 2048], P(('blk', 'dp'), 'uly')
- long_out: bfloat16 [4, 3072, 2048], P('dp', 'blk', 'uly')
Inputs may be any that keep to these rules, and one draw needn't show every extreme that they name: `short_tokens`: activations of the short bucket. `long_tokens`: activations of the long bucket; rows at or after a sequence's length are padding. `short_segments`: document numbers never fall along a sequence. `long_lengths`: a long sequence occupies positions 0 to its length - 1 of its 3072 slots.
All inputs are finite; a program needn't handle non-finite values.
Results may differ from a plain program's by a relative error of at most 0.012.
The roundings to bfloat16 on the way count: a program that leaves them out, or rounds other values in their place, can miss the bound.
Values may be sent and summed in bfloat16 or wider, within the bound.
A program may use at most 128 MiB of HBM per device.

v0:
```python
import functools
import math

import jax
import jax.numpy as jnp
from jax import lax
from jax.experimental import pallas as pl
from jax.experimental.pallas import tpu as pltpu
from jax.sharding import PartitionSpec as P

HD = 128
LONGEST_DOCUMENT = 512

masked_score = -1e30
exp2_factor = math.log2(math.e) / math.sqrt(HD)


def raw_scores(queries, keys):
    return lax.dot_general(
        queries, keys, (((1,), (1,)), ((), ())), preferred_element_type=jnp.float32
    )


def short_kernel(block_rows, col_ref, row_ref, q_ref, k_ref, v_ref, out_ref, bias_ref):
    seq_len = q_ref.shape[0]

    def window(first_row):
        return max(0, first_row - LONGEST_DOCUMENT), first_row + block_rows

    @pl.when(pl.program_id(0) == 0)
    def _():
        for first_row in range(0, seq_len, block_rows):
            low, high = window(first_row)
            shape = (block_rows, high - low)
            query_pos = first_row + lax.broadcasted_iota(jnp.int32, shape, 0)
            key_pos = low + lax.broadcasted_iota(jnp.int32, shape, 1)
            visible = (key_pos <= query_pos) & (
                col_ref[first_row : first_row + block_rows, :] == row_ref[:, low:high]
            )
            bias_ref[first_row : first_row + block_rows, low:high] = jnp.where(
                visible, 0.0, masked_score
            )

    for first_row in range(0, seq_len, block_rows):
        low, high = window(first_row)
        rows = slice(first_row, first_row + block_rows)
        scores = raw_scores(q_ref[rows, :], k_ref[low:high, :]) + bias_ref[rows, low:high]
        row_max = jnp.max(scores, axis=-1, keepdims=True)
        exponentials = jnp.exp2((scores - row_max) * exp2_factor)
        totals = jnp.sum(exponentials, axis=-1, keepdims=True)
        mixed = jnp.dot(
            exponentials.astype(jnp.bfloat16),
            v_ref[low:high, :],
            preferred_element_type=jnp.float32,
        )
        out_ref[rows, :] = (mixed / totals).astype(jnp.bfloat16)


def short_attention(projected, segments, heads, kv_heads):
    seq_len = projected.shape[0]
    group = heads // kv_heads
    block_rows = math.gcd(seq_len, 256)
    return pl.pallas_call(
        functools.partial(short_kernel, block_rows),
        grid=(heads,),
        in_specs=[
            pl.BlockSpec((seq_len, 1), lambda h: (0, 0)),
            pl.BlockSpec((1, seq_len), lambda h: (0, 0)),
            pl.BlockSpec((seq_len, HD), lambda h: (0, h)),
            pl.BlockSpec((seq_len, HD), lambda h: (0, heads + h // group)),
            pl.BlockSpec((seq_len, HD), lambda h: (0, heads + kv_heads + h // group)),
        ],
        out_specs=pl.BlockSpec((seq_len, HD), lambda h: (0, h)),
        out_shape=jax.ShapeDtypeStruct((seq_len, heads * HD), jnp.bfloat16),
        scratch_shapes=[pltpu.VMEM((seq_len, seq_len), jnp.float32)],
        cost_estimate=pl.CostEstimate(
            flops=4 * heads * seq_len * seq_len * HD,
            bytes_accessed=4 * seq_len * heads * HD,
            transcendentals=heads * seq_len * seq_len,
        ),
        compiler_params=pltpu.CompilerParams(dimension_semantics=("arbitrary",)),
    )(segments[:, None], segments[None, :], projected, projected, projected)


def long_kernel(key_rows, info_ref, q_ref, k_ref, v_ref, out_ref):
    long_count = q_ref.shape[0]
    first_pos = info_ref[0]
    long_len = info_ref[1]
    queries = q_ref[...]
    query_pos = first_pos + lax.broadcasted_iota(jnp.int32, (long_count, 1), 0)
    last_key = jnp.minimum(query_pos, long_len - 1)

    def update(block, states, masked):
        running_max, running_sum, accumulated = states
        start = pl.multiple_of(block * key_rows, key_rows)
        scores = raw_scores(queries, k_ref[pl.ds(start, key_rows), :])
        if masked:
            key_pos = start + lax.broadcasted_iota(jnp.int32, (long_count, key_rows), 1)
            scores = jnp.where(key_pos <= last_key, scores, masked_score)
        new_max = jnp.maximum(running_max, jnp.max(scores, axis=-1, keepdims=True))
        rescale = jnp.exp2((running_max - new_max) * exp2_factor)
        exponentials = jnp.exp2((scores - new_max) * exp2_factor)
        running_sum = running_sum * rescale + jnp.sum(exponentials, axis=-1, keepdims=True)
        accumulated = accumulated * rescale + jnp.dot(
            exponentials.astype(jnp.bfloat16),
            v_ref[pl.ds(start, key_rows), :],
            preferred_element_type=jnp.float32,
        )
        return new_max, running_sum, accumulated

    @pl.when(first_pos >= long_len)
    def _():
        out_ref[...] = jnp.zeros_like(out_ref)

    @pl.when(first_pos < long_len)
    def _():
        whole = jnp.minimum(first_pos + 1, long_len) // key_rows
        used = (jnp.minimum(first_pos + long_count, long_len) + key_rows - 1) // key_rows
        states = (
            jnp.full((long_count, 1), masked_score, jnp.float32),
            jnp.zeros((long_count, 1), jnp.float32),
            jnp.zeros((long_count, HD), jnp.float32),
        )
        states = lax.fori_loop(0, whole, lambda i, s: update(i, s, False), states)
        states = lax.fori_loop(whole, used, lambda i, s: update(i, s, True), states)
        running_max, running_sum, accumulated = states
        mixed = jnp.where(query_pos < long_len, accumulated / running_sum, 0.0)
        out_ref[...] = mixed.astype(jnp.bfloat16)


def long_attention(queries, kv_rows, first_pos, long_len, kv_heads):
    long_count = queries.shape[0]
    heads = queries.shape[1] // HD
    total_rows = kv_rows.shape[0]
    group = heads // kv_heads
    key_rows = math.gcd(total_rows, 768)
    return pl.pallas_call(
        functools.partial(long_kernel, key_rows),
        grid_spec=pltpu.PrefetchScalarGridSpec(
            num_scalar_prefetch=1,
            grid=(heads,),
            in_specs=[
                pl.BlockSpec((long_count, HD), lambda h, info: (0, h)),
                pl.BlockSpec((total_rows, HD), lambda h, info: (0, h // group)),
                pl.BlockSpec((total_rows, HD), lambda h, info: (0, kv_heads + h // group)),
            ],
            out_specs=pl.BlockSpec((long_count, HD), lambda h, info: (0, h)),
        ),
        out_shape=jax.ShapeDtypeStruct((long_count, heads * HD), jnp.bfloat16),
        cost_estimate=pl.CostEstimate(
            flops=4 * heads * long_count * total_rows * HD,
            bytes_accessed=4 * total_rows * kv_heads * HD,
            transcendentals=heads * long_count * total_rows,
        ),
        compiler_params=pltpu.CompilerParams(dimension_semantics=("arbitrary",)),
    )(jnp.stack([first_pos, long_len]), queries, kv_rows, kv_rows)


def project(rows, weight):
    return jnp.dot(rows, weight, preferred_element_type=jnp.float32).astype(jnp.bfloat16)


def local(short_tokens, short_segments, long_tokens, long_lengths, w_query, w_key, w_value):
    short_rows = short_tokens[0]
    long_rows = long_tokens[0]
    long_count = long_rows.shape[0]
    query_cols = w_query.shape[1]
    heads, kv_heads = query_cols // HD, w_key.shape[1] // HD
    weights = lax.all_gather(
        jnp.concatenate([w_query, w_key, w_value], axis=1), ("blk", "dp"), axis=0, tiled=True
    )
    kv_long = project(long_rows, weights[:, query_cols:])
    kv_whole = lax.all_gather(kv_long, "blk", axis=0, tiled=True)
    whole_rows = lax.all_gather(short_rows, "uly", axis=0, tiled=True)
    short_projected = project(whole_rows, weights)
    query_long = project(long_rows, weights[:, :query_cols])
    attended = short_attention(short_projected, short_segments[0], heads, kv_heads)
    short_back = lax.all_to_all(attended, "uly", split_axis=0, concat_axis=1, tiled=True)
    first_pos = lax.axis_index("blk").astype(jnp.int32) * long_count
    mixed = long_attention(query_long, kv_whole, first_pos, long_lengths[0], kv_heads)
    return short_back[None], mixed[None]


MESH = pl.DeviceIdType.MESH


def fused_kernel(
    dims, len_ref, segcol_in, segrow_in, short_ref, long_ref, wq_ref, wk_ref, wv_ref,
    short_out, long_out,
    x, w, proj, far_kv, bias, staged, segcol, segrow,
    z_send, z_recv, x_send, x_recv, y_send, y_recv, dx_send, dx_recv, dy_send, dy_recv,
    own_sem, sib_send, sib_recv, tok_sem, tok_send, tok_recv, seg_sem, seg_send, seg_recv,
    kv_send, kv_recv, out_sem, out_send, out_recv, total, highest,
):
    planes, short_len, long_count, groups, pairs, rows_step = dims
    per_group = 1 + pairs
    steps = groups * per_group
    plane_first = steps - 1
    both_short, both_long = 2 * short_len, 2 * long_count
    half_q, half_kv = groups * pairs * 2 * HD, groups * HD

    b, z = lax.axis_index("blk"), lax.axis_index("dp")
    core, chip = b % 2, b // 2
    cx, cy = chip % 2, chip // 2
    sib = b + 1 - 2 * core
    bx = b + 2 - 4 * cx
    by = b + 4 - 8 * cy
    bd = bx + by - b
    chip_x, chip_y = bx // 2, by // 2

    def z_at(k):
        return (z + k) % planes

    def remote(src, dst, send, recv, blk, dp=None):
        where = {"blk": blk} if dp is None else {"dp": dp}
        return pltpu.make_async_remote_copy(
            src_ref=src, dst_ref=dst, send_sem=send, recv_sem=recv,
            device_id=where, device_id_type=MESH,
        )

    barrier = pltpu.get_barrier_semaphore()
    for peer in (sib, bx, by, bd):
        pl.semaphore_signal(barrier, inc=1, device_id={"blk": peer}, device_id_type=MESH)
    for k in range(1, planes):
        pl.semaphore_signal(barrier, inc=1, device_id={"dp": z_at(k)}, device_id_type=MESH)
    pl.semaphore_wait(barrier, 4 + planes - 1)

    def weight_parts(p, half):
        g, r = p // per_group, p % per_group
        if r == 0:
            return ((wk_ref, half * half_kv + g * HD), (wv_ref, half * half_kv + g * HD))
        q = half * half_q + (g * pairs + r - 1) * 2 * HD
        return ((wq_ref, q), (wq_ref, q + HD))

    def own_weight(p, part):
        ref, col = weight_parts(p, core)[part]
        return pltpu.make_async_copy(
            ref.at[:, pl.ds(pl.multiple_of(col, HD), HD)],
            w.at[p, chip, core, z, :, pl.ds(part * HD, HD)],
            own_sem.at[p, part],
        )

    def sib_weight(p, part):
        ref, col = weight_parts(p, 1 - core)[part]
        return remote(
            ref.at[:, pl.ds(pl.multiple_of(col, HD), HD)],
            w.at[p, chip, core, z, :, pl.ds(part * HD, HD)],
            sib_send.at[p, part], sib_recv.at[p, part], sib,
        )

    def sib_weight_wait(p, part):
        dst = w.at[p, chip, 1 - core, z, :, pl.ds(part * HD, HD)]
        remote(dst, dst, sib_send.at[p, part], sib_recv.at[p, part], sib).wait_recv()

    def z_copy(p, k):
        unit = w.at[p, chip, :, z]
        return remote(unit, unit, z_send.at[p, k - 1], z_recv.at[p, k - 1], None, z_at(k))

    def z_wait(p, k):
        unit = w.at[p, chip, :, z_at(planes - k)]
        remote(unit, unit, z_send.at[p, k - 1], z_recv.at[p, k - 1], None, z_at(k)).wait_recv()

    def x_copy(p, zi, owner):
        unit = w.at[p, owner, :, zi]
        return remote(unit, unit, x_send.at[p, zi], x_recv.at[p, zi], bx)

    def y_copy(p, zi, owner):
        unit = w.at[p, owner, :, zi]
        return remote(unit, unit, y_send.at[p, zi], y_recv.at[p, zi], by)

    def dy_copy(p, zi, owner):
        unit = w.at[p, owner, 0, zi]
        return remote(unit, unit, dy_send.at[p, zi], dy_recv.at[p, zi], by)

    def dx_copy(p, zi, owner):
        unit = w.at[p, owner, 1, zi]
        return remote(unit, unit, dx_send.at[p, zi], dx_recv.at[p, zi], bx)

    def send_column(p, zi):
        x_copy(p, zi, chip).start()
        y_copy(p, zi, chip).start()

    def serve_z(p, k):
        z_wait(p, k)
        send_column(p, z_at(planes - k))

    def serve_diagonal(p, zi):
        x_copy(p, zi, chip_x).wait_recv()
        dy_copy(p, zi, chip_x).start()
        y_copy(p, zi, chip_y).wait_recv()
        dx_copy(p, zi, chip_y).start()

    chip_d = bd // 2

    def plane_copy(k):
        plane = w.at[plane_first, :, :, z]
        return remote(plane, plane, z_send.at[plane_first, k - 1], z_recv.at[plane_first, k - 1], None, z_at(k))

    def arrived(p):
        @pl.when(p < plane_first)
        def _():
            for zi in range(planes):
                dy_copy(p, zi, chip_d).wait_recv()
                dx_copy(p, zi, chip_d).wait_recv()

        @pl.when(p == plane_first)
        def _():
            for k in range(1, planes):
                plane = w.at[plane_first, :, :, z_at(planes - k)]
                remote(
                    plane, plane, z_send.at[plane_first, k - 1], z_recv.at[plane_first, k - 1], None, z_at(k)
                ).wait_recv()

    tokens = (
        (short_ref, pl.multiple_of(core * short_len, short_len), short_len),
        (long_ref, pl.multiple_of(both_short + core * long_count, 128), long_count),
    )
    sib_start = (
        pl.multiple_of((1 - core) * short_len, short_len),
        pl.multiple_of(both_short + (1 - core) * long_count, 128),
    )

    def token_copy(i):
        ref, start, count = tokens[i]
        return pltpu.make_async_copy(ref, x.at[pl.ds(start, count)], tok_sem.at[i])

    def token_remote(i):
        ref, start, count = tokens[i]
        return remote(ref, x.at[pl.ds(start, count)], tok_send.at[i], tok_recv.at[i], sib)

    def token_wait(i):
        dst = x.at[pl.ds(sib_start[i], tokens[i][2])]
        remote(dst, dst, tok_send.at[i], tok_recv.at[i], sib).wait_recv()

    segs = ((segcol_in, segcol), (segrow_in, segrow))

    def seg_copy(i):
        return pltpu.make_async_copy(segs[i][0], segs[i][1].at[core], seg_sem.at[i])

    def seg_remote(i):
        return remote(segs[i][0], segs[i][1].at[core], seg_send.at[i], seg_recv.at[i], sib)

    def seg_wait(i):
        dst = segs[i][1].at[1 - core]
        remote(dst, dst, seg_send.at[i], seg_recv.at[i], sib).wait_recv()

    kv_peers = ((bx, chip_x, cx == 0, cx == 1), (by, chip_y, cy == 0, cy == 1), (bd, chip_d, cy == 0, cy == 1))

    def kv_copy(g, i, owner):
        rows = far_kv.at[g, pl.ds(pl.multiple_of(owner * both_long, 128), both_long)]
        src = proj.at[g, pl.ds(both_short, both_long)]
        return remote(src, rows, kv_send.at[g, i], kv_recv.at[g, i], kv_peers[i][0])

    for p in range(steps):
        for part in range(2):
            own_weight(p, part).start()
            sib_weight(p, part).start()
    for i in range(2):
        seg_copy(i).start()
        seg_remote(i).start()
    for i in range(2):
        token_copy(i).start()
        token_remote(i).start()
    for p in range(steps):
        for part in range(2):
            own_weight(p, part).wait()
            sib_weight_wait(p, part)
        if p < plane_first:
            for k in range(1, planes):
                z_copy(p, k).start()
        send_column(p, z)

    for i in range(2):
        seg_copy(i).wait()
        seg_wait(i)

    block_rows = math.gcd(short_len, 256)
    blocks = [
        (first, max(0, first - LONGEST_DOCUMENT), first + block_rows)
        for first in range(0, short_len, block_rows)
    ]

    @pl.loop(0, 2)
    def _(s):
        for n, (first, low, high) in enumerate(blocks):
            shape = (block_rows, high - low)
            query_pos = first + lax.broadcasted_iota(jnp.int32, shape, 0)
            key_pos = low + lax.broadcasted_iota(jnp.int32, shape, 1)
            visible = (key_pos <= query_pos) & (
                segcol[s, first : first + block_rows, :] == segrow[s, :, low:high]
            )
            bias[s, n, :, : high - low] = jnp.where(visible, 0.0, masked_score)

    def serve_column(p):
        for k in range(1, planes):
            serve_z(p, k)

    def serve_diagonals(p):
        for zi in range(planes):
            serve_diagonal(p, zi)

    serve_column(0)
    serve_diagonals(0)
    serve_diagonal(plane_first, z)
    serve_column(1)
    dy_copy(plane_first, z, chip_d).wait_recv()
    dx_copy(plane_first, z, chip_d).wait_recv()
    for i in range(2):
        token_copy(i).wait()
        token_wait(i)

    row_blocks = (both_short + both_long) // rows_step
    long_block = math.gcd(both_long, 256)
    first_pos = chip * both_long

    def out_copies(q):
        slot = q % 2
        col = pl.multiple_of(core * half_q + q * 2 * HD, HD)
        mine_short = staged.at[slot, pl.ds(tokens[0][1], short_len)]
        mine_long = staged.at[slot, pl.ds(tokens[1][1], long_count)]
        other_short = staged.at[slot, pl.ds(sib_start[0], short_len)]
        other_long = staged.at[slot, pl.ds(sib_start[1], long_count)]
        to_short = short_out.at[:, pl.ds(col, 2 * HD)]
        to_long = long_out.at[:, pl.ds(col, 2 * HD)]
        return (
            pltpu.make_async_copy(mine_short, to_short, out_sem.at[slot, 0]),
            pltpu.make_async_copy(mine_long, to_long, out_sem.at[slot, 1]),
            remote(other_short, to_short, out_send.at[slot, 0], out_recv.at[q, 0], sib),
            remote(other_long, to_long, out_send.at[slot, 1], out_recv.at[q, 1], sib),
        )

    def out_wait_sent(q):
        near_short, near_long, far_short, far_long = out_copies(q)
        near_short.wait()
        near_long.wait()
        far_short.wait_send()
        far_long.wait_send()

    ones = jnp.ones((1, HD), jnp.bfloat16)

    def mix(exponentials, values):
        wide = jnp.concatenate([values, jnp.broadcast_to(ones, values.shape)], axis=1)
        return jnp.dot(exponentials.astype(jnp.bfloat16), wide, preferred_element_type=jnp.float32)

    def two_heads(rows):
        return jnp.concatenate([proj[groups, rows, :HD], proj[groups, rows, HD:]], axis=0)

    def store_heads(slot, rows, result):
        count = result.shape[0] // 2
        staged[slot, rows, :HD] = result[:count]
        staged[slot, rows, HD:] = result[count:]

    def short_pair(g, s, slot):
        base = s * short_len
        for n, (first, low, high) in enumerate(blocks):
            rows = pl.ds(pl.multiple_of(base + first, 128), block_rows)
            keys = pl.ds(pl.multiple_of(base + low, 128), high - low)
            scores = raw_scores(two_heads(rows), proj[g, keys, :HD])
            hidden = bias[s, n, :, : high - low]
            scores = scores + jnp.concatenate([hidden, hidden], axis=0)
            row_max = jnp.max(scores, axis=-1, keepdims=True)
            mixed = mix(jnp.exp2((scores - row_max) * exp2_factor), proj[g, keys, HD:])
            store_heads(slot, rows, (mixed[:, :HD] / mixed[:, HD:]).astype(jnp.bfloat16))

    long_parts = both_long // long_block

    def long_rows(n):
        return pl.ds(both_short + n * long_block, long_block)

    def long_pair(g, slot):
        shape = (long_block, long_block)
        causal = lax.broadcasted_iota(jnp.int32, shape, 1) <= lax.broadcasted_iota(jnp.int32, shape, 0)
        hidden = jnp.where(causal, 0.0, masked_score)
        hidden = jnp.concatenate([hidden, hidden], axis=0)
        for n in range(long_parts):
            seen = (n + 1) * long_block
            keys = pl.ds(both_short, seen)
            scores = raw_scores(two_heads(long_rows(n)), proj[g, keys, :HD])
            last = scores[:, seen - long_block :] + hidden
            if n:
                last = jnp.concatenate([scores[:, : seen - long_block], last], axis=1)
            row_max = jnp.max(last, axis=-1, keepdims=True)
            total[n] = mix(jnp.exp2((last - row_max) * exp2_factor), proj[g, keys, HD:])
            highest[n] = jnp.broadcast_to(row_max, highest.shape[1:])

        @pl.loop(0, chip)
        def _(block):
            far = pl.ds(pl.multiple_of(block * both_long, 128), both_long)
            for n in range(long_parts):
                scores = raw_scores(two_heads(long_rows(n)), far_kv[g, far, :HD])
                old_max = highest[n]
                new_max = jnp.maximum(old_max, jnp.max(scores, axis=-1, keepdims=True))
                rescale = jnp.exp2((old_max - new_max) * exp2_factor)
                exponentials = jnp.exp2((scores - new_max[:, :1]) * exp2_factor)
                added = mix(exponentials, far_kv[g, far, HD:])
                total[n] = total[n] * jnp.concatenate([rescale, rescale], axis=1) + added
                highest[n] = new_max

        long_len = len_ref[core * 0]
        for n in range(long_parts):
            query_pos = first_pos + n * long_block + lax.broadcasted_iota(jnp.int32, (long_block, 1), 0)
            real = jnp.where(query_pos < long_len, 1.0, 0.0)
            mixed = total[n]
            result = jnp.where(jnp.concatenate([real, real], axis=0) > 0.0, mixed[:, :HD] / mixed[:, HD:], 0.0)
            store_heads(slot, long_rows(n), result.astype(jnp.bfloat16))

    @pl.loop(0, steps)
    def _(p):
        g, r = p // per_group, p % per_group
        arrived(p)

        @pl.loop(0, row_blocks)
        def _(i):
            rows = pl.ds(pl.multiple_of(i * rows_step, rows_step), rows_step)
            weights = w[p].reshape(-1, 2 * HD)
            result = jnp.dot(x[rows, :], weights, preferred_element_type=jnp.float32)

            @pl.when(r == 0)
            def _():
                proj[g, rows, :] = result.astype(jnp.bfloat16)

            @pl.when(r > 0)
            def _():
                proj[groups, rows, :] = result.astype(jnp.bfloat16)

        @pl.when(p + 1 < plane_first)
        def _():
            serve_diagonals(p + 1)

        @pl.when(r == 0)
        def _():
            for n, (_, _, sends, _) in enumerate(kv_peers):
                @pl.when(sends)
                def _():
                    kv_copy(g, n, chip).start()

        @pl.when(p == 0)
        def _():
            serve_column(2)

        @pl.when(p + 3 < plane_first)
        def _():
            serve_column(p + 3)

        @pl.when(p + 4 == plane_first)
        def _():
            for k in range(1, planes):
                plane_copy(k).start()

        @pl.when(r > 0)
        def _():
            q = g * pairs + r - 1
            slot = q % 2

            @pl.when(q >= 2)
            def _():
                out_wait_sent(q - 2)

            @pl.loop(0, 2)
            def _(s):
                short_pair(g, s, slot)

            @pl.when(r == 1)
            def _():
                for n, (_, owner, _, receives) in enumerate(kv_peers):
                    @pl.when(receives)
                    def _():
                        kv_copy(g, n, owner).wait_recv()

            long_pair(g, slot)

            for copy in out_copies(q):
                copy.start()

    total_q = groups * pairs

    @pl.loop(max(0, total_q - 2), total_q)
    def _(q):
        out_wait_sent(q)

    @pl.loop(0, total_q)
    def _(q):
        _, _, far_short, far_long = out_copies(q)
        far_short.wait_recv()
        far_long.wait_recv()

    for p in range(steps):
        for part in range(2):
            sib_weight(p, part).wait_send()

    for k in range(1, planes):
        plane_copy(k).wait_send()
    x_copy(plane_first, z, chip).wait_send()
    y_copy(plane_first, z, chip).wait_send()
    dy_copy(plane_first, z, chip_x).wait_send()
    dx_copy(plane_first, z, chip_y).wait_send()

    @pl.loop(0, plane_first)
    def _(p):
        for k in range(1, planes):
            z_copy(p, k).wait_send()
        for zi in range(planes):
            x_copy(p, zi, chip).wait_send()
            y_copy(p, zi, chip).wait_send()
            dy_copy(p, zi, chip_x).wait_send()
            dx_copy(p, zi, chip_y).wait_send()

    for i in range(2):
        token_remote(i).wait_send()
        seg_remote(i).wait_send()
    for g in range(groups):
        for n, (_, _, sends, _) in enumerate(kv_peers):
            @pl.when(sends)
            def _():
                kv_copy(g, n, chip).wait_send()


def fused_local(planes, short_tokens, short_segments, long_tokens, long_lengths, w_query, w_key, w_value):
    short_rows, long_rows, segments = short_tokens[0], long_tokens[0], short_segments[0]
    short_len, width = short_rows.shape
    long_count = long_rows.shape[0]
    heads, kv_heads = w_query.shape[1] // HD, w_key.shape[1] // HD
    groups, pairs = kv_heads // 2, heads // kv_heads // 2
    steps = groups * (1 + pairs)
    depth = w_query.shape[0]
    chips = width // (depth * 2 * planes)
    total_rows = 2 * (short_len + long_count)
    rows_step = math.gcd(total_rows, 1408)
    block_rows = math.gcd(short_len, 256)
    long_block = math.gcd(2 * long_count, 256)
    widest = min(short_len, LONGEST_DOCUMENT + block_rows)
    dims = (planes, short_len, long_count, groups, pairs, rows_step)
    dma = pltpu.SemaphoreType.DMA
    bf16 = jnp.bfloat16
    any_space = pl.BlockSpec(memory_space=pl.ANY)
    short, long = pl.pallas_call(
        functools.partial(fused_kernel, dims),
        in_specs=[pl.BlockSpec(memory_space=pltpu.SMEM)] + [any_space] * 7,
        out_specs=[any_space] * 2,
        out_shape=[
            jax.ShapeDtypeStruct((short_len, heads * HD), bf16),
            jax.ShapeDtypeStruct((long_count, heads * HD), bf16),
        ],
        scratch_shapes=[
            pltpu.VMEM((total_rows, width), bf16),
            pltpu.VMEM((steps, chips, 2, planes, depth, 2 * HD), bf16),
            pltpu.VMEM((groups + 1, total_rows, 2 * HD), bf16),
            pltpu.VMEM((groups, chips * 2 * long_count, 2 * HD), bf16),
            pltpu.VMEM((2, short_len // block_rows, block_rows, widest), jnp.float32),
            pltpu.VMEM((2, total_rows, 2 * HD), bf16),
            pltpu.VMEM((2, short_len, 1), jnp.int32),
            pltpu.VMEM((2, 1, short_len), jnp.int32),
            dma((steps, planes - 1)), dma((steps, planes - 1)),
            dma((steps, planes)), dma((steps, planes)),
            dma((steps, planes)), dma((steps, planes)),
            dma((steps, planes)), dma((steps, planes)),
            dma((steps, planes)), dma((steps, planes)),
            dma((steps, 2)), dma((steps, 2)), dma((steps, 2)),
            dma((2,)), dma((2,)), dma((2,)),
            dma((2,)), dma((2,)), dma((2,)),
            dma((groups, 3)), dma((groups, 3)),
            dma((2, 2)), dma((2, 2)), dma((groups * pairs, 2)),
            pltpu.VMEM((2 * long_count // long_block, 2 * long_block, 2 * HD), jnp.float32),
            pltpu.VMEM((2 * long_count // long_block, 2 * long_block, HD), jnp.float32),
        ],
        compiler_params=pltpu.CompilerParams(
            collective_id=0, has_side_effects=True, vmem_limit_bytes=67043328
        ),
    )(long_lengths, segments[:, None], segments[None, :], short_rows, long_rows, w_query, w_key, w_value)
    return short[None], long[None]


def solution(mesh):
    planes = mesh.shape["dp"]
    fused = mesh.shape["blk"] == 8 and mesh.shape["uly"] == 1 and planes > 1
    return jax.shard_map(
        functools.partial(fused_local, planes) if fused else local,
        mesh=mesh,
        in_specs=(
            P(("blk", "dp"), "uly", None),
            P(("blk", "dp"), None),
            P("dp", "blk", None),
            P("dp"),
            P(("blk", "dp"), "uly"),
            P(("blk", "dp"), "uly"),
            P(("blk", "dp"), "uly"),
        ),
        out_specs=(P(("blk", "dp"), "uly", None), P("dp", "blk", "uly")),
        check_vma=False,
    )
```

profile of v0, /device:TPU:31, one launch (start us, length us, event | category | flops | bytes accessed | tf_op | source)
XLA Modules:
  0.0 182.7 jit_solution(12642675280461515884)
XLA Ops:
  1.3 1.7 copy.9.segcol_in
  3.0 173.7 %shard_map.86 = (bf16[1024,2048]{1,0:T(8,128)(2,1)}, bf16[384,2048]{1,0:T(8,128)(2,1)}) custom-call(s32[1]{0:T(128)S(6)} %copy.12.len_ref, s32[1024,1]{1,0:T(8,128)} %copy.9.segcol_in, s32[1,1024]{1,0:T(1,128)} %segrow_in.1, bf16[1024,4096]{1,0:T(8,128)(2,1)} %bitcast.5, bf16[384,4096]{1,0:T(8,128)(2,1)} %bitcast.7, bf16[128,2048]{1,0:T(8,128)(2,1)} %wq_ref.1, ...), custom_call_target="tpu_custom_call" | custom-call | tf_op jit(solution)/shard_map/pallas_call | solution.py:636
  176.7 0.0 copy-start
  176.7 4.9 %copy.13 = bf16[1,1024,2048]{2,1,0:T(8,128)(2,1)} copy(bf16[1,1024,2048]{2,1,0:T(8,128)(2,1)} %bitcast.6) | data formatting | bytes 8388608
  181.6 0.0 copy-done
  181.6 1.1 copy.14
Async XLA Ops:
  176.7 4.9 %copy-start = (bf16[384,2048]{1,0:T(8,128)(2,1)S(1)}, bf16[384,2048]{1,0:T(8,128)(2,1)}, u32[]{:S(2)}) copy-start(bf16[384,2048]{1,0:T(8,128)(2,1)} %get-tuple-element.5) | copy-start | bytes 4718596
where the time goes:
time: 183 us
  Pallas kernels  174 us (95%)
  local copies, waits for them, and re-layouts  7.76 us (4%)
    pallas_call x1, Pallas kernels, fused_local(): pl.pallas_call(functools.partial(fused_kernel, dims), in_specs=[pl.BlockS...  174 us
    unnamed x4, local copies, waits for them, and re-layouts  6.05 us

commit v1 on v0

--- a/solution.py
+++ b/solution.py
@@ -509,6 +509,10 @@
         g, r = p // per_group, p % per_group
         arrived(p)
 
+        @pl.when((p >= 2) & (p + 1 < plane_first))
+        def _():
+            serve_diagonals(p + 1)
+
         @pl.loop(0, row_blocks)
         def _(i):
             rows = pl.ds(pl.multiple_of(i * rows_step, rows_step), rows_step)
@@ -523,7 +527,7 @@
             def _():
                 proj[groups, rows, :] = result.astype(jnp.bfloat16)
 
-        @pl.when(p + 1 < plane_first)
+        @pl.when((p < 2) & (p + 1 < plane_first))
         def _():
             serve_diagonals(p + 1)
 

time: 183 us -> 177 us (0.967)
  Pallas kernels: 174 us -> 168 us
    pallas_call x1, Pallas kernels: 174 us -> 168 us  [fused_local(): pl.pallas_call(functools.partial(fused_kernel, dims), in_specs=[pl.BlockS...]
where the time goes in v1:
time: 177 us
  Pallas kernels  168 us (95%)
  local copies, waits for them, and re-layouts  7.76 us (4%)
    pallas_call x1, Pallas kernels, fused_local(): pl.pallas_call(functools.partial(fused_kernel, dims), in_specs=[pl.BlockS...  168 us
    unnamed x4, local copies, waits for them, and re-layouts  6.05 us

profile of v1, /device:TPU:31, one launch (start us, length us, event | category | flops | bytes accessed | tf_op | source)
XLA Modules:
  0.0 177.2 jit_solution(13626495358467671140)
XLA Ops:
  1.3 1.7 copy.9.segcol_in
  3.0 168.2 %shard_map.86 = (bf16[1024,2048]{1,0:T(8,128)(2,1)}, bf16[384,2048]{1,0:T(8,128)(2,1)}) custom-call(s32[1]{0:T(128)S(6)} %copy.12.len_ref, s32[1024,1]{1,0:T(8,128)} %copy.9.segcol_in, s32[1,1024]{1,0:T(1,128)} %segrow_in.1, bf16[1024,4096]{1,0:T(8,128)(2,1)} %bitcast.5, bf16[384,4096]{1,0:T(8,128)(2,1)} %bitcast.7, bf16[128,2048]{1,0:T(8,128)(2,1)} %wq_ref.1, ...), custom_call_target="tpu_custom_call" | custom-call | tf_op jit(solution)/shard_map/pallas_call | solution.py:640
  171.2 0.0 copy-start
  171.2 4.9 %copy.13 = bf16[1,1024,2048]{2,1,0:T(8,128)(2,1)} copy(bf16[1,1024,2048]{2,1,0:T(8,128)(2,1)} %bitcast.6) | data formatting | bytes 8388608
  176.1 0.0 copy-done
  176.1 1.1 copy.14
Async XLA Ops:
  171.2 4.9 %copy-start = (bf16[384,2048]{1,0:T(8,128)(2,1)S(1)}, bf16[384,2048]{1,0:T(8,128)(2,1)}, u32[]{:S(2)}) copy-start(bf16[384,2048]{1,0:T(8,128)(2,1)} %get-tuple-element.5) | copy-start | bytes 4718596
